TPU v7x, 32 devices: a whole 2x2x4 slice. The times are simulated.
32 devices in a mesh: ctx: 16 (over z, x, core), fsdp: 2 (over y).
Axes of the slice: x: 2, y: 2, z: 4, core: 2. Of those that a mesh axis runs over, the one named last changes fastest.
Arguments:
- tokens: bfloat16 [2, 2048, 1024], P('fsdp', 'ctx'), may hold values from -6 to 6
- cotangent: bfloat16 [2, 2048, 1024], P('fsdp', 'ctx'), may hold values from -6 to 6
- gain_attn: float32 [1024], replicated, may hold values from 0.5 to 1.5
- gain_mlp: float32 [1024], replicated, may hold values from 0.5 to 1.5
- qkv_weight: bfloat16 [3072, 1024], P('fsdp'), may hold values from -2 to 2
- out_weight: bfloat16 [1024, 1024], P('fsdp'), may hold values from -0.625 to 0.625
- in_weight: bfloat16 [5248, 1024], P('fsdp'), may hold values from -0.1875 to 0.1875
- down_weight: bfloat16 [1024, 2624], P('fsdp'), may hold values from -0.125 to 0.125
Outputs:
- output: float32 [2, 2048, 1024], P('fsdp', 'ctx')
- grad_input: float32 [2, 2048, 1024], P('fsdp', 'ctx')
- grad_qkv: float32 [3072, 1024], P(('ctx', 'fsdp'))
- grad_out_proj: float32 [1024, 1024], P(('ctx', 'fsdp'))
- grad_in_proj: float32 [5248, 1024], P(('ctx', 'fsdp'))
- grad_down: float32 [1024, 2624], P(('ctx', 'fsdp'))
- grad_gain_attn: float32 [1024], P(('ctx', 'fsdp'))
- grad_gain_mlp: float32 [1024], P(('ctx', 'fsdp'))
All inputs are finite; a program needn't handle non-finite values.
Results may differ from a plain program's by a relative error of at most 0.015.
Values may be sent and summed in bfloat16 or wider, within the bound.
A program may use at most 256 MiB of HBM per device.

v0:
```python
import math
import jax
import jax.numpy as jnp
from jax import lax
from jax.sharding import PartitionSpec as P

HEAD_DIM = 64
EPSILON = 1e-05
ROPE_BASE = 160000.0


def normalize(tensor):
    centred = tensor - jnp.mean(tensor, axis=-1, keepdims=True)
    inv_std = lax.rsqrt(jnp.mean(centred * centred, axis=-1, keepdims=True) + EPSILON)
    return (centred * inv_std, inv_std)


def norm_back(grad_norm, normed, inv_std):
    return inv_std * (
        grad_norm
        - jnp.mean(grad_norm, axis=-1, keepdims=True)
        - normed * jnp.mean(grad_norm * normed, axis=-1, keepdims=True)
    )


def gelu_pair(tensor):
    cumul = 0.5 * (1.0 + jax.scipy.special.erf(tensor * 0.7071067811865476))
    density = jnp.exp(-0.5 * tensor * tensor) * 0.3989422804014327
    return (tensor * cumul, cumul + tensor * density)


def rope_tables(offset, length, head_size):
    positions = (offset + jnp.arange(length, dtype=jnp.int32)).astype(jnp.float32)
    inverse = ROPE_BASE ** (
        -jnp.arange(0, head_size, 2, dtype=jnp.int32).astype(jnp.float32) / head_size
    )
    angles = positions[:, None] * inverse[None, :]
    angles = jnp.concatenate([angles, angles], axis=-1)
    return (jnp.cos(angles)[:, None, :], jnp.sin(angles)[:, None, :])


def rotate(tensor, cos_table, sine_table):
    middle = tensor.shape[-1] // 2
    turned = jnp.concatenate([-tensor[..., middle:], tensor[..., :middle]], axis=-1)
    return tensor * cos_table + turned * sine_table


def rotate_back(gradient, cos_table, sine_table):
    middle = gradient.shape[-1] // 2
    scaled = gradient * sine_table
    turned = jnp.concatenate([scaled[..., middle:], -scaled[..., :middle]], axis=-1)
    return gradient * cos_table + turned


def rows_product(left, right):
    return lax.dot_general(
        left, right, (((1,), (1,)), ((), ())), preferred_element_type=jnp.float32
    )


def rows_contract(left, right):
    return lax.dot_general(
        left, right, (((0,), (0,)), ((), ())), preferred_element_type=jnp.float32
    )


def per_device(
    tokens, cotangent, gain_attn, gain_mlp, qkv_weight, out_weight, in_weight, down_weight
):
    f32 = jnp.float32
    bf16 = jnp.bfloat16
    qkv_full, out_full, in_full, down_full = (
        lax.all_gather(qkv_weight, "fsdp", axis=0, tiled=True),
        lax.all_gather(out_weight, "fsdp", axis=0, tiled=True),
        lax.all_gather(in_weight, "fsdp", axis=0, tiled=True),
        lax.all_gather(down_weight, "fsdp", axis=0, tiled=True),
    )
    tok_rows = tokens.shape[1]
    width = tokens.shape[2]
    hidden = down_full.shape[1]
    head_size = HEAD_DIM
    head_count = width // head_size
    scale = head_size ** (-0.5)
    offset = lax.axis_index("ctx") * tok_rows
    cos_table, sine_table = rope_tables(offset, tok_rows, head_size)
    resid = tokens[0].astype(f32)
    normed_a, inv_a = normalize(resid)
    act_a = (normed_a * gain_attn).astype(bf16)
    packed = rows_product(act_a, qkv_full)
    query_heads = rotate(
        packed[:, :width].reshape(tok_rows, head_count, head_size), cos_table, sine_table
    ).astype(bf16)
    key_heads = rotate(
        packed[:, width : 2 * width].reshape(tok_rows, head_count, head_size), cos_table, sine_table
    ).astype(bf16)
    value_send = packed[:, 2 * width :].astype(bf16)
    key_send = key_heads.reshape(tok_rows, width)
    value_heads = value_send.reshape(tok_rows, head_count, head_size)
    start_state = (
        jnp.zeros((tok_rows, head_count, head_size), f32),
        jnp.full((head_count, tok_rows), -1e30, f32),
        jnp.zeros((head_count, tok_rows), f32),
    )
    key_piece = lax.all_gather(key_send, "ctx", axis=0, tiled=True)
    value_piece = lax.all_gather(value_send, "ctx", axis=0, tiled=True)
    length = key_piece.shape[0]
    step_len = math.gcd(length, 1024)

    def attend_block(block_num, running):
        weighted, row_max, row_sum = running
        key_blk = lax.dynamic_slice_in_dim(key_piece, block_num * step_len, step_len, 0).reshape(
            step_len, head_count, head_size
        )
        value_blk = lax.dynamic_slice_in_dim(
            value_piece, block_num * step_len, step_len, 0
        ).reshape(step_len, head_count, head_size)
        scores = (
            jnp.einsum("qhd,khd->hqk", query_heads, key_blk, preferred_element_type=f32) * scale
        )
        new_max = jnp.maximum(row_max, jnp.max(scores, axis=-1))
        shrink = jnp.exp(row_max - new_max)
        weights = jnp.exp(scores - new_max[..., None])
        row_sum = row_sum * shrink + jnp.sum(weights, axis=-1)
        weighted = weighted * shrink.T[:, :, None] + jnp.einsum(
            "hqk,khd->qhd", weights.astype(bf16), value_blk, preferred_element_type=f32
        )
        return (weighted, new_max, row_sum)

    weighted, row_max, row_sum = lax.fori_loop(0, length // step_len, attend_block, start_state)
    log_sum = row_max + jnp.log(row_sum)
    mixed = (weighted / row_sum.T[:, :, None]).reshape(tok_rows, width).astype(bf16)
    middle = resid + rows_product(mixed, out_full)
    normed_m, inv_m = normalize(middle)
    act_m = (normed_m * gain_mlp).astype(bf16)
    inner = rows_product(act_m, in_full)
    gelu_val, gelu_slope = gelu_pair(inner[:, :hidden])
    gated = (gelu_val * inner[:, hidden:]).astype(bf16)
    output = middle + rows_product(gated, down_full)
    cot_rows = cotangent[0]
    grad_down = rows_contract(cot_rows, gated)
    grad_gated = jnp.dot(cot_rows, down_full, preferred_element_type=f32)
    grad_inner = jnp.concatenate(
        [grad_gated * inner[:, hidden:] * gelu_slope, grad_gated * gelu_val], axis=1
    ).astype(bf16)
    grad_in = rows_contract(grad_inner, act_m)
    grad_act_m = jnp.dot(grad_inner, in_full, preferred_element_type=f32)
    grad_gain_m = jnp.sum(grad_act_m * normed_m, axis=0)
    grad_middle = cot_rows.astype(f32) + norm_back(grad_act_m * gain_mlp, normed_m, inv_m)
    grad_mid_bf = grad_middle.astype(bf16)
    grad_out = rows_contract(grad_mid_bf, mixed)
    grad_mixed = jnp.dot(grad_mid_bf, out_full, preferred_element_type=f32).astype(bf16)
    grad_heads = grad_mixed.reshape(tok_rows, head_count, head_size)
    delta_rows = jnp.sum(
        grad_heads.astype(f32) * mixed.reshape(tok_rows, head_count, head_size).astype(f32), axis=-1
    )
    delta = delta_rows.T
    zeros_heads = jnp.zeros((tok_rows, head_count, head_size), f32)
    query_key_piece = lax.all_gather(key_send, "ctx", axis=0, tiled=True)
    query_value_piece = lax.all_gather(value_send, "ctx", axis=0, tiled=True)
    length = query_key_piece.shape[0]
    query_step_len = math.gcd(length, 1024)

    def query_grad_block(block_num, grad_query):
        key_blk = lax.dynamic_slice_in_dim(
            query_key_piece, block_num * query_step_len, query_step_len, 0
        ).reshape(query_step_len, head_count, head_size)
        value_blk = lax.dynamic_slice_in_dim(
            query_value_piece, block_num * query_step_len, query_step_len, 0
        ).reshape(query_step_len, head_count, head_size)
        scores = (
            jnp.einsum("qhd,khd->hqk", query_heads, key_blk, preferred_element_type=f32) * scale
        )
        probs = jnp.exp(scores - log_sum[..., None])
        grad_probs = jnp.einsum("qhd,khd->hqk", grad_heads, value_blk, preferred_element_type=f32)
        grad_scores = (probs * (grad_probs - delta[..., None])).astype(bf16)
        return (
            grad_query
            + jnp.einsum("hqk,khd->qhd", grad_scores, key_blk, preferred_element_type=f32) * scale
        )

    grad_query = lax.fori_loop(0, length // query_step_len, query_grad_block, zeros_heads)
    query_send = query_heads.reshape(tok_rows, width).astype(f32)
    grad_send = grad_mixed.astype(f32)
    query_piece = lax.all_gather(query_send, "ctx", axis=0, tiled=True)
    grad_piece = lax.all_gather(grad_send, "ctx", axis=0, tiled=True)
    log_piece = lax.all_gather(log_sum.T, "ctx", axis=0, tiled=True)
    delta_piece = lax.all_gather(delta_rows, "ctx", axis=0, tiled=True)
    length = query_piece.shape[0]
    key_step_len = math.gcd(length, 1024)

    def key_grad_block(block_num, running):
        grad_keys, grad_values = running
        query_blk = (
            lax.dynamic_slice_in_dim(query_piece, block_num * key_step_len, key_step_len, 0)
            .astype(bf16)
            .reshape(key_step_len, head_count, head_size)
        )
        grad_blk = (
            lax.dynamic_slice_in_dim(grad_piece, block_num * key_step_len, key_step_len, 0)
            .astype(bf16)
            .reshape(key_step_len, head_count, head_size)
        )
        log_blk = lax.dynamic_slice_in_dim(log_piece, block_num * key_step_len, key_step_len, 0).T
        delta_blk = lax.dynamic_slice_in_dim(
            delta_piece, block_num * key_step_len, key_step_len, 0
        ).T
        scores = (
            jnp.einsum("qhd,khd->hqk", query_blk, key_heads, preferred_element_type=f32) * scale
        )
        probs = jnp.exp(scores - log_blk[..., None])
        grad_values = grad_values + jnp.einsum(
            "hqk,qhd->khd", probs.astype(bf16), grad_blk, preferred_element_type=f32
        )
        grad_probs = jnp.einsum("qhd,khd->hqk", grad_blk, value_heads, preferred_element_type=f32)
        grad_scores = (probs * (grad_probs - delta_blk[..., None])).astype(bf16)
        grad_keys = (
            grad_keys
            + jnp.einsum("hqk,qhd->khd", grad_scores, query_blk, preferred_element_type=f32) * scale
        )
        return (grad_keys, grad_values)

    grad_keys, grad_values = lax.fori_loop(
        0, length // key_step_len, key_grad_block, (zeros_heads, zeros_heads)
    )
    grad_query = rotate_back(grad_query, cos_table, sine_table)
    grad_keys = rotate_back(grad_keys, cos_table, sine_table)
    grad_packed = jnp.concatenate(
        [
            grad_query.reshape(tok_rows, width),
            grad_keys.reshape(tok_rows, width),
            grad_values.reshape(tok_rows, width),
        ],
        axis=1,
    ).astype(bf16)
    grad_qkv = rows_contract(grad_packed, act_a)
    grad_act_a = jnp.dot(grad_packed, qkv_full, preferred_element_type=f32)
    grad_gain_a = jnp.sum(grad_act_a * normed_a, axis=0)
    grad_input = grad_middle + norm_back(grad_act_a * gain_attn, normed_a, inv_a)
    owned = (
        lax.psum_scatter(grad_qkv, ("ctx", "fsdp"), scatter_dimension=0, tiled=True),
        lax.psum_scatter(grad_out, ("ctx", "fsdp"), scatter_dimension=0, tiled=True),
        lax.psum_scatter(grad_in, ("ctx", "fsdp"), scatter_dimension=0, tiled=True),
        lax.psum_scatter(grad_down, ("ctx", "fsdp"), scatter_dimension=0, tiled=True),
        lax.psum_scatter(grad_gain_a, ("ctx", "fsdp"), scatter_dimension=0, tiled=True),
        lax.psum_scatter(grad_gain_m, ("ctx", "fsdp"), scatter_dimension=0, tiled=True),
    )
    return (
        output[None],
        grad_input[None],
        owned[0],
        owned[1],
        owned[2],
        owned[3],
        owned[4],
        owned[5],
    )


def solution(mesh):
    return jax.shard_map(
        per_device,
        mesh=mesh,
        in_specs=(
            P("fsdp", "ctx", None),
            P("fsdp", "ctx", None),
            P(),
            P(),
            P("fsdp", None),
            P("fsdp", None),
            P("fsdp", None),
            P("fsdp", None),
        ),
        out_specs=(
            P("fsdp", "ctx", None),
            P("fsdp", "ctx", None),
            P(("ctx", "fsdp"), None),
            P(("ctx", "fsdp"), None),
            P(("ctx", "fsdp"), None),
            P(("ctx", "fsdp"), None),
            P(("ctx", "fsdp")),
            P(("ctx", "fsdp")),
        ),
        check_vma=False,
    )
```

profile of v0, /device:TPU:14, one launch (start us, length us, event | category | flops | bytes accessed | tf_op | source)
XLA Modules:
  0.0 1275.8 jit_solution(7228493947482920155)
XLA Ops:
  9.6 80.5 %all-gather.9.cloned.1.call-done = bf16[3072,1024]{1,0:T(8,128)(2,1)} async-done(((bf16[1536,1024]{1,0:T(8,128)(2,1)}), bf16[3072,1024]{1,0:T(8,128)(2,1)}) %all-gather.9.cloned.1.call-update) | async-done | bytes 6291472 | tf_op jit(solution)/shard_map/all_gather | solution.py:73
  106.7 47.2 %all-gather.11.cloned.1.call-done = bf16[2048,1024]{1,0:T(8,128)(2,1)} async-done(((bf16[128,1024]{1,0:T(8,128)(2,1)}), bf16[2048,1024]{1,0:T(8,128)(2,1)}) %all-gather.11.cloned.1.call-update) | async-done | bytes 4194320 | tf_op jit(solution)/shard_map/all_gather | solution.py:104
  153.9 6.5 copy.63
  160.4 44.6 %all-gather.13.cloned.1.call-done = bf16[2048,1024]{1,0:T(8,128)(2,1)} async-done(((bf16[128,1024]{1,0:T(8,128)(2,1)}), bf16[2048,1024]{1,0:T(8,128)(2,1)}) %all-gather.13.cloned.1.call-update) | async-done | bytes 4194320 | tf_op jit(solution)/shard_map/all_gather | solution.py:105
  205.0 6.5 copy.64
  211.5 29.9 %while.48 = (s32[]{:T(128)}, f32[128,16,64]{0,2,1:T(8,128)S(1)}, f32[16,128]{1,0:T(8,128)S(1)}, f32[16,128]{1,0:T(8,128)S(1)}, bf16[2048,1024]{0,1:T(8,128)(2,1)...) while((s32[]{:T(128)}, f32[128,16,64]{0,2,1:T(8,128)S(1)}, ...), condition=%wide.region_5.0_spmd.clone, body=%wide.region_2.0_spmd.clone.sunk | while | flops 554053632 | bytes 72745168 | solution.py:129
  244.3 127.5 %all-gather.17.cloned.1.call-done = bf16[5248,1024]{1,0:T(8,128)(2,1)} async-done(((bf16[2624,1024]{1,0:T(8,128)(2,1)}), bf16[5248,1024]{1,0:T(8,128)(2,1)}) %all-gather.17.cloned.1.call-update) | async-done | bytes 10747920 | tf_op jit(solution)/shard_map/all_gather | solution.py:75
  371.8 9.3 fusion.87
  381.1 62.2 %all-gather.19.cloned.1.call-done = bf16[1024,2624]{0,1:T(8,128)(2,1)} async-done(((bf16[512,2624]{0,1:T(8,128)(2,1)}), bf16[1024,2624]{0,1:T(8,128)(2,1)}) %all-gather.19.cloned.1.call-update) | async-done | bytes 5373968 | tf_op jit(solution)/shard_map/all_gather | solution.py:76
  448.6 7.1 multiply_reduce_fusion
  460.0 7.7 convolution_bitcast_fusion
  467.7 12.1 copy.78
  483.0 15.4 %all_gather.39 = f32[2048,16]{0,1:T(8,128)S(1)} all-gather(f32[128,16]{0,1:T(8,128)S(1)} %bitcast.218), channel_id=1, replica_groups=mesh['ctx'=16,'fsdp'=2] {'ctx'}, dimensions={0}, use_global_device_ids=true | all-gather | bytes 139264 | tf_op jit(solution)/shard_map/all_gather | solution.py:186
  499.5 22.1 %all_gather.41 = f32[2048,16]{0,1:T(8,128)S(1)} all-gather(f32[128,16]{0,1:T(8,128)S(1)} %multiply_reduce_fusion.1), channel_id=1, replica_groups=mesh['ctx'=16,'fsdp'=2] {'ctx'}, dimensions={0}, use_global_device_ids=true | all-gather | bytes 139264 | tf_op jit(solution)/shard_map/all_gather | solution.py:187
  521.6 33.4 %while.49 = (s32[]{:T(128)}, f32[128,16,64]{0,2,1:T(8,128)}, bf16[2048,1024]{0,1:T(8,128)(2,1)}, bf16[128,16,64]{0,2,1:T(8,128)(2,1)S(1)}, f32[16,128]{1,0:T(8,1...) while((s32[]{:T(128)}, f32[128,16,64]{0,2,1:T(8,128)}, ...), condition=%wide.region_12.0_spmd.clone, body=%wide.region_11.0_spmd.clone.sunk | while | flops 816185344 | bytes 33079508 | solution.py:181
  530.2 8.1 fusion.157
  546.9 8.0 fusion.157
  555.0 65.2 %while.50 = (s32[]{:T(128)}, f32[128,16,64]{0,2,1:T(8,128)}, f32[128,16,64]{0,2,1:T(8,128)S(1)}, bf16[2048,1024]{1,0:T(8,128)(2,1)}, bf16[128,16,64]{0,2,1:T(8,1...) while((s32[]{:T(128)}, f32[128,16,64]{0,2,1:T(8,128)}, ...), condition=%wide.region_14.0_spmd.clone, body=%wide.region_13.0_spmd.clone.sunk | while | flops 1091174400 | bytes 53412036 | solution.py:222
  571.4 10.8 fusion.166
  603.9 10.8 fusion.166
  630.8 9.2 fusion.50
  640.0 547.2 %fusion = f32[168,1024]{1,0:T(8,128)} fusion(f32[5248,1024]{1,0:T(8,128)} %fusion.50), kind=kCustom, calls=%all-reduce-scatter | all-reduce-scatter fusion | flops 5505025 | bytes 22183936
  1197.4 8.4 collective-permute-done
  1213.9 52.7 %all-reduce.4 = (f32[1024]{0:T(1024)S(1)}, f32[1024]{0:T(1024)S(1)}) all-reduce(f32[1024]{0:T(1024)S(1)} %get-tuple-element.613, f32[1024]{0:T(1024)S(1)} %copy-done.43), channel_id=6, replica_groups=mesh['ctx'=16,'fsdp'=2] {'ctx','fsdp'}, use_global_device_ids=true, to_apply=%region_22.0.clone | all-reduce | flops 2048 | bytes 16384
  (208 shorter events, 156.4 us)
Async XLA Ops:
  7.2 82.9 %copy-start.29 = (f32[1024]{0:T(1024)S(1)}, f32[1024]{0:T(1024)}, u32[]{:S(2)}) copy-start(f32[1024]{0:T(1024)} %param.16) | copy-start | bytes 12292
  7.2 82.9 %all-gather.9.cloned.1.call-start = ((), (), s32[]{:S(2)}) async-start(), calls=%async_computation.3 | async-start | bytes 9437184 | tf_op jit(solution)/shard_map/all_gather | solution.py:73
  7.9 146.0 %all-gather.11.cloned.1.call-start = ((), (), s32[]{:S(2)}) async-start(), calls=%async_computation.4 | async-start | bytes 4456448 | tf_op jit(solution)/shard_map/all_gather | solution.py:104
  8.2 89.4 %copy-start.25 = (f32[128,64]{0,1:T(8,128)}, f32[128,64]{0,1:T(8,128)S(1)}, u32[]{:S(2)}) copy-start(f32[128,64]{0,1:T(8,128)S(1)} %get-tuple-element.704) | copy-start | bytes 98308
  8.2 89.4 %copy-start.27 = (f32[128,64]{0,1:T(8,128)}, f32[128,64]{0,1:T(8,128)S(1)}, u32[]{:S(2)}) copy-start(f32[128,64]{0,1:T(8,128)S(1)} %get-tuple-element.703) | copy-start | bytes 98308
  9.3 85.8 %copy-start.35 = (f32[128]{0:T(128)}, f32[128]{0:T(128)S(1)}, u32[]{:S(2)}) copy-start(f32[128]{0:T(128)S(1)} %broadcast_multiply_fusion.8) | copy-start | bytes 1540
  9.6 85.5 %copy-start.37 = (f32[128]{0:T(128)}, f32[128]{0:T(128)S(1)}, u32[]{:S(2)}) copy-start(f32[128]{0:T(128)S(1)} %add_rsqrt_fusion.1) | copy-start | bytes 1540
  103.3 101.7 %all-gather.13.cloned.1.call-start = ((), (), s32[]{:S(2)}) async-start(), calls=%async_computation.5 | async-start | bytes 4456448 | tf_op jit(solution)/shard_map/all_gather | solution.py:105
  104.1 137.4 %all-gather.15.cloned.1.call-start = ((), (), s32[]{:S(2)}) async-start(), calls=%async_computation.6 | async-start | bytes 3145728 | tf_op jit(solution)/shard_map/all_gather | solution.py:74
  104.7 267.1 %all-gather.17.cloned.1.call-start = ((), (), s32[]{:S(2)}) async-start(), calls=%async_computation.7 | async-start | bytes 16121856 | tf_op jit(solution)/shard_map/all_gather | solution.py:75
  105.3 338.0 %all-gather.19.cloned.1.call-start = ((), (), s32[]{:S(2)}) async-start(), calls=%async_computation.8 | async-start | bytes 8060928 | tf_op jit(solution)/shard_map/all_gather | solution.py:76
  105.9 449.1 %all-gather.21.cloned.1.call-start = ((), (), s32[]{:S(2)}) async-start(), calls=%async_computation.9 | async-start | bytes 4456448 | tf_op jit(solution)/shard_map/all_gather | solution.py:184
  106.6 448.3 %all-gather.23.cloned.1.call-start = ((), (), s32[]{:S(2)}) async-start(), calls=%async_computation.10 | async-start | bytes 4456448 | tf_op jit(solution)/shard_map/all_gather | solution.py:185
  241.4 130.4 %copy-start.31 = (f32[1024]{0:T(1024)S(1)}, f32[1024]{0:T(1024)}, u32[]{:S(2)}) copy-start(f32[1024]{0:T(1024)} %param.17) | copy-start | bytes 12292
  244.0 211.6 %copy-start.1 = (f32[128,1024]{1,0:T(8,128)}, f32[128,1024]{1,0:T(8,128)S(1)}, u32[]{:S(2)}) copy-start(f32[128,1024]{1,0:T(8,128)S(1)} %get-tuple-element.706) | copy-start | bytes 1572868
  244.1 211.6 %copy-start.39 = (f32[128]{0:T(128)}, f32[128]{0:T(128)S(1)}, u32[]{:S(2)}) copy-start(f32[128]{0:T(128)S(1)} %broadcast_multiply_fusion.7) | copy-start | bytes 1540
  244.3 211.4 %copy-start.41 = (f32[128]{0:T(128)}, f32[128]{0:T(128)S(1)}, u32[]{:S(2)}) copy-start(f32[128]{0:T(128)S(1)} %add_rsqrt_fusion) | copy-start | bytes 1540
  244.3 199.0 %copy-start.20 = (bf16[1,128,1024]{2,1,0:T(8,128)(2,1)S(1)}, bf16[1,128,1024]{2,1,0:T(8,128)(2,1)}, u32[]{:S(2)}) copy-start(bf16[1,128,1024]{2,1,0:T(8,128)(2,1)} %param.15) | copy-start | bytes 786436
  457.1 811.7 %reduce-scatter.10.cloned.1.call-start = ((), (), s32[]{:S(2)}) async-start(), calls=%async_computation.12 | async-start | bytes 4325376 | tf_op jit(solution)/shard_map/reduce_scatter | solution.py:241
  460.0 808.9 %reduce-scatter.12.cloned.1.call-start = ((), (), s32[]{:S(2)}) async-start(), calls=%async_computation.13 | async-start | bytes 11354112
  479.8 789.0 %reduce-scatter.8.cloned.1.call-start = ((), (), s32[]{:S(2)}) async-start(), calls=%async_computation.11 | async-start | bytes 12976128 | tf_op jit(solution)/shard_map/reduce_scatter | solution.py:240
  555.0 65.3 %copy-start.28 = (f32[128,64]{0,1:T(8,128)S(1)}, f32[128,64]{0,1:T(8,128)}, u32[]{:S(2)}) copy-start(f32[128,64]{0,1:T(8,128)} %copy-done.27) | copy-start | bytes 98308
  640.0 552.9 %copy-start.3 = (f32[128,5248]{1,0:T(8,128)S(1)}, f32[128,5248]{1,0:T(8,128)}, u32[]{:S(2)}) copy-start(f32[128,5248]{1,0:T(8,128)} %fusion.87) | copy-start | bytes 8060932
  1189.1 16.7 %collective-permute-start = (f32[124,1024]{1,0:T(8,128)}, f32[124,1024]{1,0:T(8,128)}, u32[]{:S(2)}, u32[]{:S(2)}) collective-permute-start(f32[124,1024]{1,0:T(8,128)} %slice.67), channel_id=1, source_target_pairs={{0,1},{1,2},{2,3},{3,4},{4,5},{5,6},{6,7},{7,8},{8,9},{9,10},{10,1... | collective-permute-start | bytes 1523720
  (34 other events, 205.7 us)
Sparse Core Ops, SparseCore 0:
  9.5 80.5 all-gather.8
  103.4 50.4 all-gather.10
  156.1 48.8 all-gather.12
  206.4 31.5 all-gather.14
  239.4 132.3 all-gather.16
  373.2 70.0 all-gather.18
  445.4 50.5 all-gather.20
  498.1 49.5 all-gather.22
  550.6 139.3 reduce-scatter.9
  696.4 204.9 reduce-scatter.11
  908.0 196.3 reduce-scatter.7
where the time goes:
time: 1280 us
  blocking collectives  637 us (50%)
  waiting for transfers between devices  373 us (29%)
  matrix products  152 us (12%)
  local copies, waits for them, and re-layouts  82 us (6%)
  between operations  15 us (1%)
    unnamed x2, blocking collectives  600 us
    all_gather x1, waiting for transfers between devices, per_device(): lax.all_gather(in_weight, 'fsdp', axis=0, tiled=True)  128 us
    all_gather x1, waiting for transfers between devices, per_device(): lax.all_gather(qkv_weight, 'fsdp', axis=0, tiled=True)  80.5 us
    all_gather x1, waiting for transfers between devices, per_device(): lax.all_gather(down_weight, 'fsdp', axis=0, tiled=True)  62.2 us
    all_gather x1, waiting for transfers between devices, per_device(): key_piece = lax.all_gather(key_send, 'ctx', axis=0, tiled=True)  47.2 us
    all_gather x1, waiting for transfers between devices, per_device(): value_piece = lax.all_gather(value_send, 'ctx', axis=0, tiled=True)  44.6 us
    unnamed x92, local copies, waits for them, and re-layouts  36 us
    dot_general x4, matrix products, rows_contract(): lax.dot_general(left, right, (((0,), (0,)), ((), ())), preferred_element_...  26 us
  transfers between devices with their start and end apart: 12, of which 6 were waited for; matrix products, arithmetic and copies ran while one was open for 61% of the time, Pallas kernels for 0%

commit v1 on v0

--- a/solution.py
+++ b/solution.py
@@ -101,8 +101,11 @@
         jnp.full((head_count, tok_rows), -1e30, f32),
         jnp.zeros((head_count, tok_rows), f32),
     )
-    key_piece = lax.all_gather(key_send, "ctx", axis=0, tiled=True)
-    value_piece = lax.all_gather(value_send, "ctx", axis=0, tiled=True)
+    key_piece, value_piece = jnp.split(
+        lax.all_gather(jnp.concatenate([key_send, value_send], axis=1), "ctx", axis=0, tiled=True),
+        [key_send.shape[1]],
+        axis=1,
+    )
     length = key_piece.shape[0]
     step_len = math.gcd(length, 1024)
 

time: 1280 us -> 1360 us (1.062)
  waiting for transfers between devices: 373 us -> 410 us
  local copies, waits for them, and re-layouts: 82 us -> 108 us
    all_gather x1, waiting for transfers between devices: 0.01 us -> 51.1 us  [per_device(): grad_piece = lax.all_gather(grad_send, 'ctx', axis=0, tiled=True)]
    all_gather x1, waiting for transfers between devices: 128 us -> 105 us  [per_device(): lax.all_gather(in_weight, 'fsdp', axis=0, tiled=True)]
    unnamed x92 -> x94, local copies, waits for them, and re-layouts: 36 us -> 23 us
    all_gather x2 -> x3, waiting for transfers between devices: 91.9 us -> 96.2 us  [the longest x1 70.2 us: per_device(): lax.all_gather(jnp.concatenate([key_send, value_send], axis=1), 'ctx', ax...]
  transfers between devices with their start and end apart: 12 -> 13, of which waited for: 6 -> 8; matrix products, arithmetic and copies ran while one was open for 61% -> 60% of each run, Pallas kernels for 0% -> 0%
where the time goes in v1:
time: 1360 us; the launch traced here: 1350 us
  blocking collectives  641 us (47%)
  waiting for transfers between devices  410 us (30%)
  matrix products  158 us (12%)
  local copies, waits for them, and re-layouts  108 us (8%)
  between operations  15.3 us (1%)
    unnamed x2, blocking collectives  604 us
    all_gather x1, waiting for transfers between devices, per_device(): lax.all_gather(in_weight, 'fsdp', axis=0, tiled=True)  105 us
    all_gather x1, waiting for transfers between devices, per_device(): lax.all_gather(qkv_weight, 'fsdp', axis=0, tiled=True)  80.5 us
    all_gather x1, waiting for transfers between devices, per_device(): lax.all_gather(jnp.concatenate([key_send, value_send], axis=1), 'ctx', ax...  70.2 us
    all_gather x1, waiting for transfers between devices, per_device(): lax.all_gather(down_weight, 'fsdp', axis=0, tiled=True)  62.2 us
    all_gather x1, waiting for transfers between devices, per_device(): grad_piece = lax.all_gather(grad_send, 'ctx', axis=0, tiled=True)  51.1 us
  transfers between devices with their start and end apart: 13, of which 8 were waited for; matrix products, arithmetic and copies ran while one was open for 60% of the time, Pallas kernels for 0%

profile of v1, /device:TPU:14, one launch (start us, length us, event | category | flops | bytes accessed | tf_op | source)
XLA Modules:
  0.0 1349.5 jit_solution(487884915991531751)
XLA Ops:
  9.6 80.5 %all-gather.10.cloned.1.call-done = bf16[3072,1024]{1,0:T(8,128)(2,1)} async-done(((bf16[1536,1024]{1,0:T(8,128)(2,1)}), bf16[3072,1024]{1,0:T(8,128)(2,1)}) %all-gather.10.cloned.1.call-update) | async-done | bytes 6291472 | tf_op jit(solution)/shard_map/all_gather | solution.py:73
  109.1 70.2 %all-gather.12.cloned.1.call-done = bf16[2048,2048]{1,0:T(8,128)(2,1)} async-done(((bf16[128,2048]{1,0:T(8,128)(2,1)}), bf16[2048,2048]{1,0:T(8,128)(2,1)}) %all-gather.12.cloned.1.call-update) | async-done | bytes 8388624 | tf_op jit(solution)/shard_map/all_gather | solution.py:105
  185.2 53.3 %while.48 = (s32[]{:T(128)}, f32[128,16,64]{0,2,1:T(8,128)S(1)}, f32[16,128]{1,0:T(8,128)S(1)}, f32[16,128]{1,0:T(8,128)S(1)}, bf16[2048,1024]{1,0:T(8,128)(2,1)...) while((s32[]{:T(128)}, f32[128,16,64]{0,2,1:T(8,128)S(1)}, ...), condition=%wide.region_5.0_spmd.clone, body=%wide.region_2.0_spmd.clone.sunk | while | flops 554053632 | bytes 81133776 | solution.py:132
  222.0 7.7 bitcast_reduce_fusion.2
  241.4 105.2 %all-gather.16.cloned.1.call-done = bf16[5248,1024]{1,0:T(8,128)(2,1)} async-done(((bf16[2624,1024]{1,0:T(8,128)(2,1)}), bf16[5248,1024]{1,0:T(8,128)(2,1)}) %all-gather.16.cloned.1.call-update) | async-done | bytes 10747920 | tf_op jit(solution)/shard_map/all_gather | solution.py:75
  346.6 9.2 fusion.87
  355.8 62.2 %all-gather.18.cloned.1.call-done = bf16[1024,2624]{0,1:T(8,128)(2,1)} async-done(((bf16[512,2624]{0,1:T(8,128)(2,1)}), bf16[1024,2624]{0,1:T(8,128)(2,1)}) %all-gather.18.cloned.1.call-update) | async-done | bytes 5373968 | tf_op jit(solution)/shard_map/all_gather | solution.py:76
  423.4 7.1 multiply_reduce_fusion
  434.8 7.7 convolution_bitcast_fusion
  442.5 12.0 copy.78
  457.7 15.4 %all_gather.41 = f32[2048,16]{0,1:T(8,128)S(1)} all-gather(f32[128,16]{0,1:T(8,128)S(1)} %bitcast.218), channel_id=1, replica_groups=mesh['ctx'=16,'fsdp'=2] {'ctx'}, dimensions={0}, use_global_device_ids=true | all-gather | bytes 139264 | tf_op jit(solution)/shard_map/all_gather | solution.py:189
  474.2 22.1 %all_gather.43 = f32[2048,16]{0,1:T(8,128)S(1)} all-gather(f32[128,16]{0,1:T(8,128)S(1)} %multiply_reduce_fusion.1), channel_id=1, replica_groups=mesh['ctx'=16,'fsdp'=2] {'ctx'}, dimensions={0}, use_global_device_ids=true | all-gather | bytes 139264 | tf_op jit(solution)/shard_map/all_gather | solution.py:190
  496.3 26.1 %all-gather.22.cloned.1.call-done = bf16[2048,1024]{1,0:T(8,128)(2,1)} async-done(((bf16[128,1024]{1,0:T(8,128)(2,1)}), bf16[2048,1024]{1,0:T(8,128)(2,1)}) %all-gather.22.cloned.1.call-update) | async-done | bytes 4194320 | tf_op jit(solution)/shard_map/all_gather | solution.py:162
  522.4 48.5 %while.49 = (s32[]{:T(128)}, f32[128,16,64]{0,2,1:T(8,128)}, bf16[2048,1024]{1,0:T(8,128)(2,1)}, bf16[128,16,64]{0,2,1:T(8,128)(2,1)S(1)}, f32[16,128]{1,0:T(8,1...) while((s32[]{:T(128)}, f32[128,16,64]{0,2,1:T(8,128)}, ...), condition=%wide.region_12.0_spmd.clone, body=%wide.region_11.0_spmd.clone.sunk | while | flops 816185344 | bytes 41468116 | solution.py:184
  538.6 8.0 fusion.158
  562.7 8.2 fusion.158
  573.5 51.1 %all-gather.26.cloned.1.call-done = bf16[2048,1024]{1,0:T(8,128)(2,1)} async-done(((bf16[128,1024]{1,0:T(8,128)(2,1)}), bf16[2048,1024]{1,0:T(8,128)(2,1)}) %all-gather.26.cloned.1.call-update) | async-done | bytes 4194320 | tf_op jit(solution)/shard_map/all_gather | solution.py:188
  624.6 65.1 %while.50 = (s32[]{:T(128)}, f32[128,16,64]{0,2,1:T(8,128)}, f32[128,16,64]{0,2,1:T(8,128)S(1)}, bf16[2048,1024]{1,0:T(8,128)(2,1)}, bf16[128,16,64]{0,2,1:T(8,1...) while((s32[]{:T(128)}, f32[128,16,64]{0,2,1:T(8,128)}, ...), condition=%wide.region_14.0_spmd.clone, body=%wide.region_13.0_spmd.clone.sunk | while | flops 1091174400 | bytes 53412036 | solution.py:225
  641.0 10.8 fusion.167
  673.5 10.8 fusion.167
  700.4 9.2 fusion.50
  709.6 552.9 %fusion = f32[168,1024]{1,0:T(8,128)} fusion(f32[5248,1024]{1,0:T(8,128)} %fusion.50), kind=kCustom, calls=%all-reduce-scatter | all-reduce-scatter fusion | flops 5505025 | bytes 22183936
  1272.7 8.1 collective-permute-done
  1289.0 51.0 %all-reduce.4 = (f32[1024]{0:T(1024)S(1)}, f32[1024]{0:T(1024)S(1)}) all-reduce(f32[1024]{0:T(1024)S(1)} %get-tuple-element.613, f32[1024]{0:T(1024)S(1)} %copy-done.45), channel_id=6, replica_groups=mesh['ctx'=16,'fsdp'=2] {'ctx','fsdp'}, use_global_device_ids=true, to_apply=%region_22.0.clone | all-reduce | flops 2048 | bytes 16384
  (223 shorter events, 198.0 us)
Async XLA Ops:
  7.2 82.9 %copy-start.31 = (f32[1024]{0:T(1024)S(1)}, f32[1024]{0:T(1024)}, u32[]{:S(2)}) copy-start(f32[1024]{0:T(1024)} %param.16) | copy-start | bytes 12292
  7.2 82.9 %all-gather.10.cloned.1.call-start = ((), (), s32[]{:S(2)}) async-start(), calls=%async_computation.3 | async-start | bytes 9437184 | tf_op jit(solution)/shard_map/all_gather | solution.py:73
  7.9 171.4 %all-gather.12.cloned.1.call-start = ((), (), s32[]{:S(2)}) async-start(), calls=%async_computation.4 | async-start | bytes 8912896 | tf_op jit(solution)/shard_map/all_gather | solution.py:105
  8.2 89.5 %copy-start.27 = (f32[128,64]{0,1:T(8,128)}, f32[128,64]{0,1:T(8,128)S(1)}, u32[]{:S(2)}) copy-start(f32[128,64]{0,1:T(8,128)S(1)} %get-tuple-element.706) | copy-start | bytes 98308
  8.2 89.5 %copy-start.29 = (f32[128,64]{0,1:T(8,128)}, f32[128,64]{0,1:T(8,128)S(1)}, u32[]{:S(2)}) copy-start(f32[128,64]{0,1:T(8,128)S(1)} %get-tuple-element.705) | copy-start | bytes 98308
  9.3 80.7 %copy-start.37 = (f32[128]{0:T(128)}, f32[128]{0:T(128)S(1)}, u32[]{:S(2)}) copy-start(f32[128]{0:T(128)S(1)} %broadcast_multiply_fusion.8) | copy-start | bytes 1540
  105.1 133.5 %all-gather.14.cloned.1.call-start = ((), (), s32[]{:S(2)}) async-start(), calls=%async_computation.5 | async-start | bytes 3145728 | tf_op jit(solution)/shard_map/all_gather | solution.py:74
  105.8 240.8 %all-gather.16.cloned.1.call-start = ((), (), s32[]{:S(2)}) async-start(), calls=%async_computation.6 | async-start | bytes 16121856 | tf_op jit(solution)/shard_map/all_gather | solution.py:75
  106.4 311.6 %all-gather.18.cloned.1.call-start = ((), (), s32[]{:S(2)}) async-start(), calls=%async_computation.7 | async-start | bytes 8060928 | tf_op jit(solution)/shard_map/all_gather | solution.py:76
  107.0 389.3 %all-gather.20.cloned.1.call-start = ((), (), s32[]{:S(2)}) async-start(), calls=%async_computation.8 | async-start | bytes 4456448 | tf_op jit(solution)/shard_map/all_gather | solution.py:161
  107.6 414.8 %all-gather.22.cloned.1.call-start = ((), (), s32[]{:S(2)}) async-start(), calls=%async_computation.9 | async-start | bytes 4456448 | tf_op jit(solution)/shard_map/all_gather | solution.py:162
  108.3 465.2 %all-gather.24.cloned.1.call-start = ((), (), s32[]{:S(2)}) async-start(), calls=%async_computation.10 | async-start | bytes 4456448 | tf_op jit(solution)/shard_map/all_gather | solution.py:187
  109.1 515.5 %all-gather.26.cloned.1.call-start = ((), (), s32[]{:S(2)}) async-start(), calls=%async_computation.11 | async-start | bytes 4456448 | tf_op jit(solution)/shard_map/all_gather | solution.py:188
  238.5 108.1 %copy-start.33 = (f32[1024]{0:T(1024)S(1)}, f32[1024]{0:T(1024)}, u32[]{:S(2)}) copy-start(f32[1024]{0:T(1024)} %param.17) | copy-start | bytes 12292
  241.1 189.4 %copy-start.1 = (f32[128,1024]{1,0:T(8,128)}, f32[128,1024]{1,0:T(8,128)S(1)}, u32[]{:S(2)}) copy-start(f32[128,1024]{1,0:T(8,128)S(1)} %get-tuple-element.708) | copy-start | bytes 1572868
  241.1 189.3 %copy-start.41 = (f32[128]{0:T(128)}, f32[128]{0:T(128)S(1)}, u32[]{:S(2)}) copy-start(f32[128]{0:T(128)S(1)} %broadcast_multiply_fusion.7) | copy-start | bytes 1540
  241.3 189.1 %copy-start.43 = (f32[128]{0:T(128)}, f32[128]{0:T(128)S(1)}, u32[]{:S(2)}) copy-start(f32[128]{0:T(128)S(1)} %add_rsqrt_fusion) | copy-start | bytes 1540
  241.4 176.7 %copy-start.22 = (bf16[1,128,1024]{2,1,0:T(8,128)(2,1)S(1)}, bf16[1,128,1024]{2,1,0:T(8,128)(2,1)}, u32[]{:S(2)}) copy-start(bf16[1,128,1024]{2,1,0:T(8,128)(2,1)} %param.15) | copy-start | bytes 786436
  432.0 910.2 %reduce-scatter.10.cloned.1.call-start = ((), (), s32[]{:S(2)}) async-start(), calls=%async_computation.13 | async-start | bytes 4325376 | tf_op jit(solution)/shard_map/reduce_scatter | solution.py:244
  434.8 907.4 %reduce-scatter.12.cloned.1.call-start = ((), (), s32[]{:S(2)}) async-start(), calls=%async_computation.14 | async-start | bytes 11354112
  454.5 887.7 %reduce-scatter.8.cloned.1.call-start = ((), (), s32[]{:S(2)}) async-start(), calls=%async_computation.12 | async-start | bytes 12976128 | tf_op jit(solution)/shard_map/reduce_scatter | solution.py:243
  522.4 102.2 %copy-start.6 = (bf16[128,16,64]{0,2,1:T(8,128)(2,1)S(1)}, bf16[128,16,64]{0,2,1:T(8,128)(2,1)}, u32[]{:S(2)}) copy-start(bf16[128,16,64]{0,2,1:T(8,128)(2,1)} %get-tuple-element.921) | copy-start | bytes 786436
  709.6 558.6 %copy-start.3 = (f32[128,5248]{1,0:T(8,128)S(1)}, f32[128,5248]{1,0:T(8,128)}, u32[]{:S(2)}) copy-start(f32[128,5248]{1,0:T(8,128)} %fusion.87) | copy-start | bytes 8060932
  1264.5 16.4 %collective-permute-start = (f32[124,1024]{1,0:T(8,128)}, f32[124,1024]{1,0:T(8,128)}, u32[]{:S(2)}, u32[]{:S(2)}) collective-permute-start(f32[124,1024]{1,0:T(8,128)} %slice.67), channel_id=1, source_target_pairs={{0,1},{1,2},{2,3},{3,4},{4,5},{5,6},{6,7},{7,8},{8,9},{9,10},{10,1... | collective-permute-start | bytes 1523720
  (37 other events, 327.0 us)
Sparse Core Ops, SparseCore 0:
  9.5 80.5 all-gather.9
  105.2 74.0 all-gather.11
  180.8 31.9 all-gather.13
  214.2 132.3 all-gather.15
  348.0 70.0 all-gather.17
  420.1 50.4 all-gather.19
  472.8 49.5 all-gather.21
  524.6 48.8 all-gather.23
  575.7 48.9 all-gather.25
  627.3 144.3 reduce-scatter.9
  778.2 207.4 reduce-scatter.11
  992.2 193.7 reduce-scatter.7
